TPU v7x, 32 devices: a whole 2x2x4 slice. The times are simulated.
32 devices in a mesh: member: 4 (over y, x), region: 2 (over core), block: 4 (over z).
Axes of the slice: x: 2, y: 2, z: 4, core: 2. Of those that a mesh axis runs over, the one named last changes fastest.
Arguments:
- traffic_load: float32 [128, 65536], P('member', ('region', 'block')), may hold values from 0.05 to 0.7
- free_speed: float32 [65536], P(('region', 'block')), may hold values from 0.3 to 0.95
- wave_speed: float32 [65536], P(('region', 'block')), may hold values from 0.15 to 0.6
- jam_density: float32 [65536], P(('region', 'block')), may hold values from 0.8 to 1.2
- capacity_share: float32 [65536], P(('region', 'block')), may hold values from 0.5 to 1
- observation_cell: int32 [24576], P(('region', 'block')), may hold values from 0 to 2047
- obs_count: int32 [32], P(('region', 'block')), may hold values from 1 to 768, 12288 in all
- observation_value: float32 [24576], P(('region', 'block')), may hold values from 0 to 0.8
- observation_variance: float32 [24576], P(('region', 'block')), may hold values from 0.002 to 0.02
- observation_noise: float32 [128, 24576], P('member', ('region', 'block')), may hold values from -6 to 6
- block_lists: int32 [32, 3], P(('region', 'block')), may hold values from 0 to 31, as said below
Outputs:
- analysis: float32 [128, 65536], P('member', ('region', 'block'))
Inputs may be any that keep to these rules, and one draw needn't show every extreme that they name: `block_lists`: row b lists 3 different blocks, b itself among them, each within 4 blocks of b.
All inputs are finite; a program needn't handle non-finite values. No bound on the sum of `obs_count` on one device may be relied on, other than what follows from the above.
Results may differ from a plain program's by a relative error of at most 0.0003.
Values sent between devices are 32-bit elements; how exact they have to be, the bound alone decides.
A program may use at most 64 MiB of HBM per device.

v0:
```python
import jax
import jax.numpy as jnp
from jax import lax
from jax.sharding import PartitionSpec as P

REALIZATION_TALLY = 128
HORIZON_TICKS = 16
CELLS_PER_BLOCK = 2048
BLOCK_SLOTS = 768


def padded(value, sides, width):
    for axis, dim in sides:
        size, length = (lax.axis_size(axis), value.shape[dim])
        up = [(i, (i + 1) % size) for i in range(size - 1)]
        down = [(j, i) for i, j in up]
        last = lax.slice_in_dim(value, length - width, length, axis=dim)
        leading = lax.slice_in_dim(value, 0, width, axis=dim)
        before = lax.ppermute(last, axis, up)
        after = lax.ppermute(leading, axis, down)
        value = jnp.concatenate([before, value, after], axis=dim)
    return value


def road_capacity(free_speed, wave_speed, jam_density, capacity_share):
    return capacity_share * free_speed * wave_speed * jam_density / (free_speed + wave_speed)


def block_products(left_side, right_side, weight, block_total):
    member_count = left_side.shape[0]
    left_blocks = (left_side * weight).reshape(member_count, block_total, -1)
    right_blocks = right_side.reshape(member_count, block_total, -1)
    return jnp.einsum("kbo,jbo->bkj", left_blocks, right_blocks, precision=lax.Precision.HIGHEST)


def body(
    traffic_load,
    free_speed,
    wave_speed,
    jam_density,
    capacity_share,
    observation_cell,
    obs_count,
    observation_value,
    observation_variance,
    observation_noise,
    block_lists,
):
    mem_local, cell_total = traffic_load.shape
    block_total = obs_count.shape[0]
    slot_total = observation_cell.shape[0]
    capacity = road_capacity(free_speed, wave_speed, jam_density, capacity_share)
    is_last = lax.axis_index(("region", "block")) == lax.axis_size(("region", "block")) - 1
    margin = HORIZON_TICKS
    state_wide = padded(traffic_load, ((("region", "block"), 1),), margin)
    road_wide = padded(
        jnp.stack([free_speed, wave_speed, jam_density, capacity]),
        ((("region", "block"), 1),),
        margin,
    )
    speed_wide = road_wide[0]
    wave_wide = road_wide[1]
    jam_wide = road_wide[2]
    capacity_wide = road_wide[3]
    exit_mask = (jnp.arange(cell_total + 2 * margin) == cell_total + margin) & is_last
    exit_value = capacity[-1]

    def advance_wide(step_index, state):
        demand = jnp.minimum(speed_wide * state, capacity_wide)
        supply = jnp.minimum(capacity_wide, wave_wide * (jam_wide - state))
        supply = jnp.where(exit_mask[None, :], exit_value, supply)
        fluxes = jnp.minimum(demand[:, :-1], supply[:, 1:])
        updated = state[:, 1:-1] + fluxes[:, :-1] - fluxes[:, 1:]
        return state.at[:, 1:-1].set(updated)

    predicted_traffic_load = lax.fori_loop(0, HORIZON_TICKS, advance_wide, state_wide)[
        :, margin : margin + cell_total
    ]
    realization_total = lax.psum(jnp.sum(predicted_traffic_load, axis=0), "member")
    realization_average = realization_total / REALIZATION_TALLY
    realization_departure = predicted_traffic_load - realization_average
    slot_cell_index = (
        jnp.arange(slot_total, dtype=jnp.int32) // BLOCK_SLOTS * CELLS_PER_BLOCK + observation_cell
    )
    obs_anomaly = jnp.take(realization_departure, slot_cell_index, axis=1)
    obs_mean = jnp.take(realization_average, slot_cell_index)
    live_mask = (
        (jnp.arange(BLOCK_SLOTS, dtype=jnp.int32)[None, :] < obs_count[:, None])
        .reshape(-1)
        .astype(jnp.float32)
    )
    weight = live_mask / observation_variance
    misfit = observation_value - obs_mean
    obs_all, noise_all = (
        lax.all_gather(obs_anomaly, "member", axis=0, tiled=True),
        lax.all_gather(observation_noise, "member", axis=0, tiled=True),
    )
    spread = jnp.sum(obs_all * obs_all, axis=0) / (REALIZATION_TALLY - 1)
    misfit_sum, spread_sum = lax.psum(
        (
            jnp.sum(misfit * misfit * weight),
            jnp.sum(live_mask * (spread / observation_variance + 1.0)),
        ),
        ("region", "block"),
    )
    inflation = jnp.sqrt(misfit_sum / spread_sum)
    perturbed = misfit + jnp.sqrt(observation_variance) * noise_all
    scaled = inflation * obs_all
    gram_part = block_products(scaled, scaled, weight, block_total)
    cross_part = block_products(scaled, perturbed - scaled, weight, block_total)
    neighbour_pairs = padded(
        jnp.stack([gram_part, cross_part]), ((("region", "block"), 1),), block_total
    )
    first_block = (lax.axis_index(("region", "block")) - 1) * block_total
    relative = block_lists - first_block
    selector = jnp.sum(
        (
            relative[:, :, None] == jnp.arange(3 * block_total, dtype=jnp.int32)[None, None, :]
        ).astype(jnp.float32),
        axis=1,
    )
    local_gram = jnp.einsum(
        "be,ekj->bkj", selector, neighbour_pairs[0], precision=lax.Precision.HIGHEST
    )
    local_cross = jnp.einsum(
        "be,ekj->bkj", selector, neighbour_pairs[1], precision=lax.Precision.HIGHEST
    )
    identity = (REALIZATION_TALLY - 1) * jnp.eye(REALIZATION_TALLY, dtype=jnp.float32)[None]
    system = identity + local_gram
    factors = jnp.linalg.cholesky(system)
    mixing = jax.vmap(lambda factor, target: jax.scipy.linalg.cho_solve((factor, True), target))(
        factors, local_cross
    )
    member_start = lax.axis_index("member") * mem_local
    own_columns = lax.dynamic_slice_in_dim(mixing, member_start, mem_local, 2)
    row_piece = lax.all_gather(realization_departure, "member", axis=0, tiled=True)
    row_count = row_piece.shape[0]
    piece_blocks = row_piece.reshape(row_count, block_total, CELLS_PER_BLOCK)
    change = (
        jnp.zeros((mem_local, block_total, CELLS_PER_BLOCK), jnp.float32)
        + jnp.einsum("kbc,bkj->jbc", piece_blocks, own_columns, precision=lax.Precision.HIGHEST)
    ).reshape(mem_local, cell_total)
    return realization_average + inflation * realization_departure + inflation * change


def solution(mesh):
    placed = (
        P("member", ("region", "block")),
        P(("region", "block")),
        P(("region", "block")),
        P(("region", "block")),
        P(("region", "block")),
        P(("region", "block")),
        P(("region", "block")),
        P(("region", "block")),
        P(("region", "block")),
        P("member", ("region", "block")),
        P(("region", "block"), None),
    )
    return jax.shard_map(
        body,
        mesh=mesh,
        in_specs=placed,
        out_specs=P("member", ("region", "block")),
        check_vma=False,
    )
```

profile of v0, /device:TPU:0, one launch (start us, length us, event | category | flops | bytes accessed | tf_op | source)
XLA Modules:
  0.0 368.9 jit_solution(8760085229739747867)
XLA Ops:
  8.4 4.9 %collective-permute-start.2 = (f32[4,16]{1,0:T(4,128)S(1)}, f32[4,16]{1,0:T(4,128)S(1)}, u32[]{:S(2)}, u32[]{:S(2)}) collective-permute-start(f32[4,16]{1,0:T(4,128)S(1)} %get-tuple-element.210), channel_id=1, source_target_pairs={{0,1},{1,2},{2,3},{3,4},{4,5},{5,6},{6,7},{8,9},{9,10},{10,11},{11... | collective-permute-start | bytes 776 | tf_op jit(solution)/shard_map/ppermute | solution.py:19
  15.5 4.5 %collective-permute-start = (f32[32,16]{1,0:T(8,128)S(1)}, f32[32,16]{1,0:T(8,128)S(1)}, u32[]{:S(2)}, u32[]{:S(2)}) collective-permute-start(f32[32,16]{1,0:T(8,128)S(1)} %get-tuple-element.204), channel_id=1, source_target_pairs={{0,1},{1,2},{2,3},{3,4},{4,5},{5,6},{6,7},{8,9},{9,10},{10,11},{11... | collective-permute-start | bytes 6152 | tf_op jit(solution)/shard_map/ppermute | solution.py:19
  26.4 90.7 %while.15 = (s32[]{:T(128)}, f32[32,8224]{1,0:T(8,128)S(1)}, pred[]{:T(512)}, f32[1,8224]{1,0:T(1,128)S(1)}, f32[1,8224]{1,0:T(1,128)S(1)}, /*index=5*/f32[]{:T(...) while((s32[]{:T(128)}, f32[32,8224]{1,0:T(8,128)S(1)}, ...), condition=%wide.region_2.3_spmd.clone, body=%wide.region_1.0_spmd.clone.sunk | while | flops 2647714 | bytes 10195928 | solution.py:76
  28.1 1.3 fusion.48
  29.4 2.7 scatter.7
  33.8 1.3 fusion.48
  35.1 2.7 scatter.7
  39.5 1.3 fusion.48
  40.8 2.7 scatter.7
  45.1 1.3 fusion.48
  46.4 2.7 scatter.7
  50.8 1.3 fusion.48
  52.1 2.7 scatter.7
  56.5 1.3 fusion.48
  57.8 2.7 scatter.7
  63.4 2.7 scatter.7
  69.1 2.7 scatter.7
  74.8 2.7 scatter.7
  79.1 1.3 fusion.48
  80.4 2.7 scatter.7
  86.1 2.7 scatter.7
  91.8 2.7 scatter.7
  97.4 2.7 scatter.7
  103.1 2.7 scatter.7
  108.8 2.7 scatter.7
  114.5 2.7 scatter.7
  117.5 16.3 %psum.21 = f32[8192]{0:T(1024)S(1)} all-reduce(f32[8192]{0:T(1024)S(1)} %slice_reduce_fusion), channel_id=1, replica_groups=mesh['member'=4,'region'=2,'block'=4] {'member'}, use_global_device_ids=true, to_apply=%region_4.5 | all-reduce | flops 8192 | bytes 65536 | tf_op jit(solution)/shard_map/psum | solution.py:79
  134.1 2.7 copy.79
  136.8 17.4 %gather_fusion = f32[3072]{0:T(1024)S(1)} fusion(f32[8192]{0:T(1024)S(1)} %broadcast_multiply_fusion.2, s32[3072]{0:T(1024)S(1)} %broadcast_clamp_fusion), kind=kCustom, calls=%fused_computation | custom fusion | bytes 36864 | tf_op jit(solution)/shard_map/jit(_take)/gather | solution.py:86
  154.3 13.0 %gather_fusion.1 = f32[3072,32]{1,0:T(8,128)} fusion(f32[32,8192]{0,1:T(8,128)} %copy.79, s32[3072]{0:T(1024)S(1)} %broadcast_clamp_fusion), kind=kCustom, calls=%fused_computation.1 | custom fusion | bytes 798720 | tf_op jit(solution)/shard_map/jit(_take)/gather | solution.py:85
  168.0 2.7 select_bitcast_fusion
  172.7 3.1 copy.85
  175.8 27.7 %all-gather.4.cloned.1.call-done = f32[128,3072]{1,0:T(8,128)} async-done(((f32[32,3072]{1,0:T(8,128)}), f32[128,3072]{1,0:T(8,128)}) %all-gather.4.cloned.1.call-update) | async-done | bytes 1572880 | tf_op jit(solution)/shard_map/all_gather | solution.py:95
  203.5 1.7 multiply_reduce_fusion
  205.9 17.1 %all-reduce = (f32[]{:T(128)}, f32[]{:T(128)}) all-reduce(f32[]{:T(128)} %get-tuple-element.195, f32[]{:T(128)} %select_reduce_fusion.1), channel_id=1, replica_groups=mesh['member'=4,'region'=2,'block'=4] {'region','block'}, use_global_device_ids=true, to_apply=%region_6.7 | all-reduce | flops 2 | bytes 16 | tf_op jit(solution)/shard_map/psum | solution.py:99
  224.3 1.6 copy.82
  226.0 3.2 add_subtract_fusion
  229.6 2.7 convolution_bitcast_fusion.1
  232.4 2.7 convolution_bitcast_fusion
  235.1 1.7 collective-permute-start.4
  236.8 1.5 collective-permute-start.5
  238.6 10.0 %collective-permute-done.4 = f32[2,4,128,128]{3,2,1,0:T(8,128)S(1)} collective-permute-done((f32[2,4,128,128]{3,2,1,0:T(8,128)S(1)}, f32[2,4,128,128]{3,2,1,0:T(8,128)S(1)}, u32[]{:S(2)}, u32[]{:S(2)}) %collective-permute-start.4) | collective-permute-done | bytes 524320 | tf_op jit(solution)/shard_map/ppermute | solution.py:19
  248.6 10.3 %collective-permute-done.5 = f32[2,4,128,128]{3,2,1,0:T(8,128)S(1)} collective-permute-done((f32[2,4,128,128]{3,2,1,0:T(8,128)S(1)}, f32[2,4,128,128]{3,2,1,0:T(8,128)S(1)}, u32[]{:S(2)}, u32[]{:S(2)}) %collective-permute-start.5) | collective-permute-done | bytes 524320 | tf_op jit(solution)/shard_map/ppermute | solution.py:20
  260.5 46.9 %custom-call.11 = f32[4,128,128]{2,1,0:T(8,128)S(1)} custom-call(f32[4,128,128]{2,1,0:T(8,128)S(1)} %fusion.19), custom_call_target="Cholesky" | custom-call | tf_op jit(solution)/shard_map/jit(cholesky)/cholesky | solution.py:130
  307.7 39.3 %custom-call.12 = f32[4,1,128,128]{2,3,1,0:T(8,128)S(1)} custom-call(f32[4,1,128,128]{3,2,1,0:T(8,128)S(1)} %select_bitcast_fusion.1), custom_call_target="InvertDiagBlocksLowerTriangular" | custom-call | tf_op jit(solution)/shard_map/vmap(jit(_cho_solve))/triangular_solve | solution.py:131
  349.4 5.6 %copy.96 = f32[128,8192]{0,1:T(8,128)} copy(f32[128,8192]{1,0:T(8,128)} %all-gather.8.cloned.1.call-done) | data formatting | bytes 8388608 | tf_op jit(solution)/shard_map/all_gather | solution.py:136
  355.0 6.0 %fusion.9 = f32[4,4,8,2048]{3,2,1,0:T(8,128)S(1)} fusion(f32[128,4,2048]{0,2,1:T(8,128)} %bitcast.50, f32[]{:T(128)S(6)} %sqrt.6, f32[4,128,128]{1,2,0:T(8,128)S(1)} %fusion.14, s32[]{:T(128)S(6)} %select_n.38), kind=kOutput, calls=%fused_computation.16 | convolution fusion | flops 402915328 | bytes 5308424 | tf_op jit(solution)/shard_map/kbc,bkj->jbc/dot_general | solution.py:141
  361.0 1.3 add_add_fusion
  (235 shorter events, 57.3 us)
Async XLA Ops:
  6.5 19.2 %copy-start.2 = (f32[32,8192]{1,0:T(8,128)S(1)}, f32[32,8192]{1,0:T(8,128)}, u32[]{:S(2)}) copy-start(f32[32,8192]{1,0:T(8,128)} %param.15) | copy-start | bytes 3145732
  6.5 166.2 %all-gather.6.cloned.1.call-start = ((), (), s32[]{:S(2)}) async-start(), calls=%async_computation.1 | async-start | bytes 1966080 | tf_op jit(solution)/shard_map/all_gather | solution.py:96
  8.4 15.8 %collective-permute-start.2 = (f32[4,16]{1,0:T(4,128)S(1)}, f32[4,16]{1,0:T(4,128)S(1)}, u32[]{:S(2)}, u32[]{:S(2)}) collective-permute-start(f32[4,16]{1,0:T(4,128)S(1)} %get-tuple-element.210), channel_id=1, source_target_pairs={{0,1},{1,2},{2,3},{3,4},{4,5},{5,6},{6,7},{8,9},{9,10},{10,11},{11... | collective-permute-start | bytes 776 | tf_op jit(solution)/shard_map/ppermute | solution.py:19
  13.4 10.8 %collective-permute-start.3 = (f32[4,16]{1,0:T(4,128)S(1)}, f32[4,16]{1,0:T(4,128)S(1)}, u32[]{:S(2)}, u32[]{:S(2)}) collective-permute-start(f32[4,16]{1,0:T(4,128)S(1)} %get-tuple-element.209), channel_id=1, source_target_pairs={{1,0},{2,1},{3,2},{4,3},{5,4},{6,5},{7,6},{9,8},{10,9},{11,10},{12... | collective-permute-start | bytes 776 | tf_op jit(solution)/shard_map/ppermute | solution.py:20
  15.5 9.0 %collective-permute-start = (f32[32,16]{1,0:T(8,128)S(1)}, f32[32,16]{1,0:T(8,128)S(1)}, u32[]{:S(2)}, u32[]{:S(2)}) collective-permute-start(f32[32,16]{1,0:T(8,128)S(1)} %get-tuple-element.204), channel_id=1, source_target_pairs={{0,1},{1,2},{2,3},{3,4},{4,5},{5,6},{6,7},{8,9},{9,10},{10,11},{11... | collective-permute-start | bytes 6152 | tf_op jit(solution)/shard_map/ppermute | solution.py:19
  20.1 5.6 %collective-permute-start.1 = (f32[32,16]{1,0:T(8,128)S(1)}, f32[32,16]{1,0:T(8,128)S(1)}, u32[]{:S(2)}, u32[]{:S(2)}) collective-permute-start(f32[32,16]{1,0:T(8,128)S(1)} %get-tuple-element.203), channel_id=1, source_target_pairs={{1,0},{2,1},{3,2},{4,3},{5,4},{6,5},{7,6},{9,8},{10,9},{11,10},{12... | collective-permute-start | bytes 6152 | tf_op jit(solution)/shard_map/ppermute | solution.py:20
  21.4 182.1 %all-gather.4.cloned.1.call-start = ((), (), s32[]{:S(2)}) async-start(), calls=%async_computation | async-start | bytes 1966080 | tf_op jit(solution)/shard_map/all_gather | solution.py:95
  134.1 2.7 copy-start
  154.2 13.0 %copy-start.3 = (f32[3072]{0:T(1024)S(1)}, f32[3072]{0:T(1024)}, u32[]{:S(2)}) copy-start(f32[3072]{0:T(1024)} %param.23) | copy-start | bytes 36868
  154.3 13.0 %copy-start.4 = (s32[3072]{0:T(1024)S(1)}, s32[3072]{0:T(1024)}, u32[]{:S(2)}) copy-start(s32[3072]{0:T(1024)} %param.20) | copy-start | bytes 36868
  154.3 13.0 %copy-start.5 = (f32[3072]{0:T(1024)S(1)}, f32[3072]{0:T(1024)}, u32[]{:S(2)}) copy-start(f32[3072]{0:T(1024)} %param.22) | copy-start | bytes 36868
  172.0 177.4 %all-gather.8.cloned.1.call-start = ((), (), s32[]{:S(2)}) async-start(), calls=%async_computation.2 | async-start | bytes 5242880 | tf_op jit(solution)/shard_map/all_gather | solution.py:136
  203.5 20.8 %copy-start.1 = (f32[128,3072]{1,0:T(8,128)S(1)}, f32[128,3072]{1,0:T(8,128)}, u32[]{:S(2)}) copy-start(f32[128,3072]{1,0:T(8,128)} %all-gather.4.cloned.1.call-done) | copy-start | bytes 4718596
  232.3 6.0 %copy-start.6 = (s32[4,3]{1,0:T(4,128)S(1)}, s32[4,3]{1,0:T(4,128)}, u32[]{:S(2)}) copy-start(s32[4,3]{1,0:T(4,128)} %param.25) | copy-start | bytes 148
  235.1 13.5 %collective-permute-start.4 = (f32[2,4,128,128]{3,2,1,0:T(8,128)S(1)}, f32[2,4,128,128]{3,2,1,0:T(8,128)S(1)}, u32[]{:S(2)}, u32[]{:S(2)}) collective-permute-start(f32[2,4,128,128]{3,2,1,0:T(8,128)S(1)} %pad_maximum_fusion.1), channel_id=1, source_target_pairs={{0,1},{1,2},{2,3},{3,4},{4,5},{5,6},{6,7},{8,9},{9,10},{10,11},{11... | collective-permute-start | bytes 1572872 | tf_op jit(solution)/shard_map/ppermute | solution.py:19
  236.8 22.2 %collective-permute-start.5 = (f32[2,4,128,128]{3,2,1,0:T(8,128)S(1)}, f32[2,4,128,128]{3,2,1,0:T(8,128)S(1)}, u32[]{:S(2)}, u32[]{:S(2)}) collective-permute-start(f32[2,4,128,128]{3,2,1,0:T(8,128)S(1)} %pad_maximum_fusion.1), channel_id=1, source_target_pairs={{1,0},{2,1},{3,2},{4,3},{5,4},{6,5},{7,6},{9,8},{10,9},{11,10},{12... | collective-permute-start | bytes 1572872 | tf_op jit(solution)/shard_map/ppermute | solution.py:20
Sparse Core Ops, SparseCore 0:
  21.5 33.1 all-gather.5
  172.1 31.4 all-gather.3
  205.4 52.5 all-gather.7
where the time goes:
time: 370 us; the launch traced here: 369 us
  other arithmetic  144 us (39%)
  local copies, waits for them, and re-layouts  95.2 us (26%)
  waiting for transfers between devices  50 us (14%)
  blocking collectives  33.4 us (9%)
  starting transfers between devices  15.3 us (4%)
  matrix products  14.8 us (4%)
  between operations  14.8 us (4%)
    another operation x4, other arithmetic, body(): factors = jnp.linalg.cholesky(system)  47.1 us
    scatter x16, local copies, waits for them, and re-layouts, advance_wide(): return state.at[:, 1:-1].set(updated)  42.5 us
    another operation x3, other arithmetic, body(): jax.scipy.linalg.cho_solve((factor, True), target)  39.4 us
    all_gather x1, waiting for transfers between devices, body(): lax.all_gather(obs_anomaly, 'member', axis=0, tiled=True)  27.7 us
    another operation x17, other arithmetic  21.6 us
    gather x1, local copies, waits for them, and re-layouts, body(): obs_mean = jnp.take(realization_average, slot_cell_index)  17.4 us
    psum x1, blocking collectives, body(): lax.psum((jnp.sum(misfit * misfit * weight), jnp.sum(live_mask * (spread...  17.1 us
    psum x1, blocking collectives, body(): lax.psum(jnp.sum(predicted_traffic_load, axis=0), 'member')  16.3 us
  transfers between devices with their start and end apart: 9, of which 4 were waited for; matrix products, arithmetic and copies ran while one was open for 65% of the time, Pallas kernels for 0%

commit v1 on v0

--- a/solution.py
+++ b/solution.py
@@ -7,6 +7,25 @@
 HORIZON_TICKS = 16
 CELLS_PER_BLOCK = 2048
 BLOCK_SLOTS = 768
+
+
+def run_meet(inner_x, dimension_no):
+    next_value = list(inner_x.shape[1:])
+    next_value[dimension_no] *= inner_x.shape[0]
+    current_block = jnp.moveaxis(inner_x, 0, dimension_no).reshape(next_value)
+    return current_block
+
+
+def bring_leaf_all(mine_x, device_axis):
+    parts_n = lax.axis_size(device_axis)
+    long_array = mine_x[None]
+    for p in range(parts_n.bit_length() - 1):
+        value_now = 1 << p
+        r1 = lax.ppermute(long_array, device_axis, [(j0, j0 ^ value_now) for j0 in range(parts_n)])
+        z2 = jnp.stack([long_array, r1])
+        newest = lax.axis_index(device_axis) >> p & 1
+        long_array = jnp.where(newest == 0, z2, z2[::-1]).reshape(-1, *mine_x.shape)
+    return long_array
 
 
 def padded(value, sides, width):
@@ -46,6 +65,11 @@
     observation_noise,
     block_lists,
 ):
+
+    def _recover_roads(incoming_x, panel, dim_k):
+        u_next = run_meet(bring_leaf_all(incoming_x, panel), dim_k)
+        return u_next
+
     mem_local, cell_total = traffic_load.shape
     block_total = obs_count.shape[0]
     slot_total = observation_cell.shape[0]
@@ -92,7 +116,7 @@
     weight = live_mask / observation_variance
     misfit = observation_value - obs_mean
     obs_all, noise_all = (
-        lax.all_gather(obs_anomaly, "member", axis=0, tiled=True),
+        _recover_roads(obs_anomaly, "member", 0),
         lax.all_gather(observation_noise, "member", axis=0, tiled=True),
     )
     spread = jnp.sum(obs_all * obs_all, axis=0) / (REALIZATION_TALLY - 1)

time: 370 us -> 382 us (1.032)
  other arithmetic: 144 us -> 151 us
  local copies, waits for them, and re-layouts: 95.2 us -> 99.9 us
    ppermute x0 -> x2, waiting for transfers between devices: none -> 32.8 us  [bring_leaf_all(): lax.ppermute(long_array, device_axis, [(j0, j0 ^ value_now) for j0 in ran...]
    all_gather x1 -> x0, waiting for transfers between devices: 27.7 us -> none  [body(): lax.all_gather(obs_anomaly, 'member', axis=0, tiled=True)]
    another operation x17 -> x20, other arithmetic: 21.6 us -> 27.5 us
    all_gather x2 -> x0, local copies, waits for them, and re-layouts: 4.76 us -> none  [the longest x1 3.11 us: body(): lax.all_gather(observation_noise, 'member', axis=0, tiled=True)]
    ppermute x3, waiting for transfers between devices: 11.5 us -> 7.16 us  [padded(): after = lax.ppermute(leading, axis, down)]
  transfers between devices with their start and end apart: 9 -> 10, of which waited for: 4 -> 5; matrix products, arithmetic and copies ran while one was open for 65% -> 65% of each run, Pallas kernels for 0% -> 0%
where the time goes in v1:
time: 382 us; the launch traced here: 381 us
  other arithmetic  151 us (40%)
  local copies, waits for them, and re-layouts  99.9 us (26%)
  waiting for transfers between devices  50.7 us (13%)
  blocking collectives  30.8 us (8%)
  starting transfers between devices  18.6 us (5%)
  between operations  15.2 us (4%)
  matrix products  14.5 us (4%)
    another operation x4, other arithmetic, body(): factors = jnp.linalg.cholesky(system)  47.1 us
    scatter x16, local copies, waits for them, and re-layouts, advance_wide(): return state.at[:, 1:-1].set(updated)  42.5 us
    another operation x3, other arithmetic, body(): jax.scipy.linalg.cho_solve((factor, True), target)  39.4 us
    ppermute x2, waiting for transfers between devices, bring_leaf_all(): lax.ppermute(long_array, device_axis, [(j0, j0 ^ value_now) for j0 in ran...  32.8 us
    another operation x17, other arithmetic  21.6 us
    gather x1, local copies, waits for them, and re-layouts, body(): obs_mean = jnp.take(realization_average, slot_cell_index)  17.4 us
    psum x1, blocking collectives, body(): lax.psum(jnp.sum(predicted_traffic_load, axis=0), 'member')  16.3 us
    min x16, other arithmetic, advance_wide(): fluxes = jnp.minimum(demand[:, :-1], supply[:, 1:])  15.8 us
  transfers between devices with their start and end apart: 10, of which 5 were waited for; matrix products, arithmetic and copies ran while one was open for 65% of the time, Pallas kernels for 0%

profile of v1, /device:TPU:0, one launch (start us, length us, event | category | flops | bytes accessed | tf_op | source)
XLA Modules:
  0.0 381.2 jit_solution(1705997889292946786)
XLA Ops:
  8.4 4.9 %collective-permute-start.2 = (f32[4,16]{1,0:T(4,128)S(1)}, f32[4,16]{1,0:T(4,128)S(1)}, u32[]{:S(2)}, u32[]{:S(2)}) collective-permute-start(f32[4,16]{1,0:T(4,128)S(1)} %get-tuple-element.210), channel_id=1, source_target_pairs={{0,1},{1,2},{2,3},{3,4},{4,5},{5,6},{6,7},{8,9},{9,10},{10,11},{11... | collective-permute-start | bytes 776 | tf_op jit(solution)/shard_map/ppermute | solution.py:38
  15.5 4.5 %collective-permute-start = (f32[32,16]{1,0:T(8,128)S(1)}, f32[32,16]{1,0:T(8,128)S(1)}, u32[]{:S(2)}, u32[]{:S(2)}) collective-permute-start(f32[32,16]{1,0:T(8,128)S(1)} %get-tuple-element.204), channel_id=1, source_target_pairs={{0,1},{1,2},{2,3},{3,4},{4,5},{5,6},{6,7},{8,9},{9,10},{10,11},{11... | collective-permute-start | bytes 6152 | tf_op jit(solution)/shard_map/ppermute | solution.py:38
  26.4 90.7 %while.15 = (s32[]{:T(128)}, f32[32,8224]{1,0:T(8,128)S(1)}, pred[]{:T(512)}, f32[1,8224]{1,0:T(1,128)S(1)}, f32[1,8224]{1,0:T(1,128)S(1)}, /*index=5*/f32[]{:T(...) while((s32[]{:T(128)}, f32[32,8224]{1,0:T(8,128)S(1)}, ...), condition=%wide.region_2.3_spmd.clone, body=%wide.region_1.0_spmd.clone.sunk | while | flops 2647714 | bytes 10195928 | solution.py:100
  28.1 1.3 fusion.64
  29.4 2.7 scatter.7
  35.1 2.7 scatter.7
  40.8 2.7 scatter.7
  46.4 2.7 scatter.7
  52.1 2.7 scatter.7
  57.8 2.7 scatter.7
  63.4 2.7 scatter.7
  69.1 2.7 scatter.7
  74.8 2.7 scatter.7
  80.4 2.7 scatter.7
  86.1 2.7 scatter.7
  91.8 2.7 scatter.7
  97.4 2.7 scatter.7
  103.1 2.7 scatter.7
  108.8 2.7 scatter.7
  114.5 2.7 scatter.7
  117.5 16.3 %psum.21 = f32[8192]{0:T(1024)S(1)} all-reduce(f32[8192]{0:T(1024)S(1)} %slice_reduce_fusion), channel_id=1, replica_groups=mesh['member'=4,'region'=2,'block'=4] {'member'}, use_global_device_ids=true, to_apply=%region_4.5 | all-reduce | flops 8192 | bytes 65536 | tf_op jit(solution)/shard_map/psum | solution.py:103
  134.1 2.7 copy.79
  136.8 17.4 %gather_fusion = f32[3072]{0:T(1024)S(1)} fusion(f32[8192]{0:T(1024)S(1)} %broadcast_multiply_fusion.1, s32[3072]{0:T(1024)S(1)} %broadcast_clamp_fusion), kind=kCustom, calls=%fused_computation | custom fusion | bytes 36864 | tf_op jit(solution)/shard_map/jit(_take)/gather | solution.py:110
  154.3 10.3 %gather_fusion.1 = f32[3072,32]{1,0:T(8,128)S(1)} fusion(f32[32,8192]{0,1:T(8,128)} %copy.79, s32[3072]{0:T(1024)S(1)} %broadcast_clamp_fusion), kind=kCustom, calls=%fused_computation.1 | custom fusion | bytes 798720 | tf_op jit(solution)/shard_map/jit(_take)/gather | solution.py:109
  165.3 2.5 bitcast_select_fusion
  167.8 1.8 copy.80
  169.7 2.5 bitcast_select_fusion.1
  172.2 8.0 %collective-permute-done.4 = f32[1,32,3072]{2,1,0:T(8,128)S(1)} collective-permute-done((f32[1,32,3072]{2,1,0:T(8,128)S(1)}, f32[1,32,3072]{2,1,0:T(8,128)S(1)}, u32[]{:S(2)}, u32[]{:S(2)}) %collective-permute-start.4) | collective-permute-done | bytes 393248 | tf_op jit(solution)/shard_map/ppermute | solution.py:24
  180.2 1.6 copy.81
  181.8 1.6 pad_maximum_fusion
  183.4 3.0 fusion.10
  186.4 2.3 copy.82
  189.8 2.3 copy.83
  192.1 24.7 %collective-permute-done.5 = f32[2,32,3072]{2,1,0:T(8,128)S(1)} collective-permute-done((f32[2,32,3072]{2,1,0:T(8,128)S(1)}, f32[2,32,3072]{2,1,0:T(8,128)S(1)}, u32[]{:S(2)}, u32[]{:S(2)}) %collective-permute-start.5) | collective-permute-done | bytes 786464 | tf_op jit(solution)/shard_map/ppermute | solution.py:24
  219.8 14.5 %all-reduce = (f32[]{:T(128)}, f32[]{:T(128)}) all-reduce(f32[]{:T(128)} %get-tuple-element.193, f32[]{:T(128)} %select_reduce_fusion.1), channel_id=1, replica_groups=mesh['member'=4,'region'=2,'block'=4] {'region','block'}, use_global_device_ids=true, to_apply=%region_6.7 | all-reduce | flops 2 | bytes 16 | tf_op jit(solution)/shard_map/psum | solution.py:123
  235.6 1.4 fusion.19
  237.0 2.1 mul.159
  241.4 3.4 fusion.20
  244.9 1.8 bitcast_subtract_fusion
  246.8 1.7 fusion.25
  248.5 4.2 %collective-permute-start.6 = (f32[2,4,128,128]{3,2,1,0:T(8,128)S(1)}, f32[2,4,128,128]{3,2,1,0:T(8,128)S(1)}, u32[]{:S(2)}, u32[]{:S(2)}) collective-permute-start(f32[2,4,128,128]{3,2,1,0:T(8,128)S(1)} %pad_maximum_fusion.3), channel_id=1, source_target_pairs={{0,1},{1,2},{2,3},{3,4},{4,5},{5,6},{6,7},{8,9},{9,10},{10,11},{11... | collective-permute-start | bytes 1572872 | tf_op jit(solution)/shard_map/ppermute | solution.py:38
  254.3 10.7 %collective-permute-done.6 = f32[2,4,128,128]{3,2,1,0:T(8,128)S(1)} collective-permute-done((f32[2,4,128,128]{3,2,1,0:T(8,128)S(1)}, f32[2,4,128,128]{3,2,1,0:T(8,128)S(1)}, u32[]{:S(2)}, u32[]{:S(2)}) %collective-permute-start.6) | collective-permute-done | bytes 524320 | tf_op jit(solution)/shard_map/ppermute | solution.py:38
  265.0 6.0 %collective-permute-done.7 = f32[2,4,128,128]{3,2,1,0:T(8,128)S(1)} collective-permute-done((f32[2,4,128,128]{3,2,1,0:T(8,128)S(1)}, f32[2,4,128,128]{3,2,1,0:T(8,128)S(1)}, u32[]{:S(2)}, u32[]{:S(2)}) %collective-permute-start.7) | collective-permute-done | bytes 524320 | tf_op jit(solution)/shard_map/ppermute | solution.py:39
  272.6 46.9 %custom-call.11 = f32[4,128,128]{2,1,0:T(8,128)S(1)} custom-call(f32[4,128,128]{2,1,0:T(8,128)S(1)} %fusion.39), custom_call_target="Cholesky" | custom-call | tf_op jit(solution)/shard_map/jit(cholesky)/cholesky | solution.py:154
  319.8 39.3 %custom-call.12 = f32[4,1,128,128]{2,3,1,0:T(8,128)S(1)} custom-call(f32[4,1,128,128]{3,2,1,0:T(8,128)S(1)} %select_bitcast_fusion), custom_call_target="InvertDiagBlocksLowerTriangular" | custom-call | tf_op jit(solution)/shard_map/vmap(jit(_cho_solve))/triangular_solve | solution.py:155
  361.4 5.6 %copy.97 = f32[128,8192]{0,1:T(8,128)} copy(f32[128,8192]{1,0:T(8,128)} %all-gather.5.cloned.1.call-done) | data formatting | bytes 8388608 | tf_op jit(solution)/shard_map/all_gather | solution.py:160
  367.0 6.0 %fusion.11 = f32[4,4,8,2048]{3,2,1,0:T(8,128)S(1)} fusion(f32[128,4,2048]{0,2,1:T(8,128)} %bitcast.67, f32[]{:T(128)S(6)} %sqrt.6, f32[4,128,128]{1,2,0:T(8,128)S(1)} %fusion.34, s32[]{:T(128)S(6)} %select_n.75), kind=kOutput, calls=%fused_computation.20 | convolution fusion | flops 402915328 | bytes 5308424 | tf_op jit(solution)/shard_map/kbc,bkj->jbc/dot_general | solution.py:165
  373.1 1.3 add_add_fusion
  (255 shorter events, 69.6 us)
Async XLA Ops:
  6.5 19.2 %copy-start.6 = (f32[32,8192]{1,0:T(8,128)S(1)}, f32[32,8192]{1,0:T(8,128)}, u32[]{:S(2)}) copy-start(f32[32,8192]{1,0:T(8,128)} %param.15) | copy-start | bytes 3145732
  6.5 238.3 %all-gather.3.cloned.1.call-start = ((), (), s32[]{:S(2)}) async-start(), calls=%async_computation | async-start | bytes 1966080 | tf_op jit(solution)/shard_map/all_gather | solution.py:120
  8.4 15.8 %collective-permute-start.2 = (f32[4,16]{1,0:T(4,128)S(1)}, f32[4,16]{1,0:T(4,128)S(1)}, u32[]{:S(2)}, u32[]{:S(2)}) collective-permute-start(f32[4,16]{1,0:T(4,128)S(1)} %get-tuple-element.210), channel_id=1, source_target_pairs={{0,1},{1,2},{2,3},{3,4},{4,5},{5,6},{6,7},{8,9},{9,10},{10,11},{11... | collective-permute-start | bytes 776 | tf_op jit(solution)/shard_map/ppermute | solution.py:38
  13.4 10.8 %collective-permute-start.3 = (f32[4,16]{1,0:T(4,128)S(1)}, f32[4,16]{1,0:T(4,128)S(1)}, u32[]{:S(2)}, u32[]{:S(2)}) collective-permute-start(f32[4,16]{1,0:T(4,128)S(1)} %get-tuple-element.209), channel_id=1, source_target_pairs={{1,0},{2,1},{3,2},{4,3},{5,4},{6,5},{7,6},{9,8},{10,9},{11,10},{12... | collective-permute-start | bytes 776 | tf_op jit(solution)/shard_map/ppermute | solution.py:39
  15.5 9.0 %collective-permute-start = (f32[32,16]{1,0:T(8,128)S(1)}, f32[32,16]{1,0:T(8,128)S(1)}, u32[]{:S(2)}, u32[]{:S(2)}) collective-permute-start(f32[32,16]{1,0:T(8,128)S(1)} %get-tuple-element.204), channel_id=1, source_target_pairs={{0,1},{1,2},{2,3},{3,4},{4,5},{5,6},{6,7},{8,9},{9,10},{10,11},{11... | collective-permute-start | bytes 6152 | tf_op jit(solution)/shard_map/ppermute | solution.py:38
  20.1 5.6 %collective-permute-start.1 = (f32[32,16]{1,0:T(8,128)S(1)}, f32[32,16]{1,0:T(8,128)S(1)}, u32[]{:S(2)}, u32[]{:S(2)}) collective-permute-start(f32[32,16]{1,0:T(8,128)S(1)} %get-tuple-element.203), channel_id=1, source_target_pairs={{1,0},{2,1},{3,2},{4,3},{5,4},{6,5},{7,6},{9,8},{10,9},{11,10},{12... | collective-permute-start | bytes 6152 | tf_op jit(solution)/shard_map/ppermute | solution.py:39
  21.4 340.0 %all-gather.5.cloned.1.call-start = ((), (), s32[]{:S(2)}) async-start(), calls=%async_computation.1 | async-start | bytes 5242880 | tf_op jit(solution)/shard_map/all_gather | solution.py:160
  134.1 2.7 copy-start.4
  154.2 10.4 %copy-start.8 = (f32[3072]{0:T(1024)S(1)}, f32[3072]{0:T(1024)}, u32[]{:S(2)}) copy-start(f32[3072]{0:T(1024)} %param.23) | copy-start | bytes 36868
  154.3 10.4 %copy-start.9 = (s32[3072]{0:T(1024)S(1)}, s32[3072]{0:T(1024)}, u32[]{:S(2)}) copy-start(s32[3072]{0:T(1024)} %param.20) | copy-start | bytes 36868
  154.3 10.4 %copy-start.10 = (f32[3072]{0:T(1024)S(1)}, f32[3072]{0:T(1024)}, u32[]{:S(2)}) copy-start(f32[3072]{0:T(1024)} %param.22) | copy-start | bytes 36868
  169.6 10.6 %collective-permute-start.4 = (f32[1,32,3072]{2,1,0:T(8,128)S(1)}, f32[1,32,3072]{2,1,0:T(8,128)S(1)}, u32[]{:S(2)}, u32[]{:S(2)}) collective-permute-start(f32[1,32,3072]{2,1,0:T(8,128)S(1)} %copy.80), channel_id=1, source_target_pairs={{0,8},{8,0},{16,24},{24,16},{1,9},{9,1},{17,25},{25,17},{2,10},{10... | collective-permute-start | bytes 1179656 | tf_op jit(solution)/shard_map/ppermute | solution.py:24
  172.2 9.7 %copy-start.5 = (f32[1,1,32,3072]{2,3,1,0:T(8,128)S(1)}, f32[1,1,32,3072]{2,3,1,0:T(8,128)}, u32[]{:S(2)}) copy-start(f32[1,1,32,3072]{2,3,1,0:T(8,128)} %bitcast_select_fusion.1) | copy-start | bytes 1179652
  188.8 28.1 %collective-permute-start.5 = (f32[2,32,3072]{2,1,0:T(8,128)S(1)}, f32[2,32,3072]{2,1,0:T(8,128)S(1)}, u32[]{:S(2)}, u32[]{:S(2)}) collective-permute-start(f32[2,32,3072]{2,1,0:T(8,128)S(1)} %copy.82), channel_id=1, source_target_pairs={{0,16},{8,24},{16,0},{24,8},{1,17},{9,25},{17,1},{25,9},{2,18},{10... | collective-permute-start | bytes 2359304 | tf_op jit(solution)/shard_map/ppermute | solution.py:24
  216.8 0.9 copy-start.7
  239.0 1.2 copy-start.1
  240.2 1.2 copy-start.2
  241.4 3.5 copy-start
  244.9 1.9 copy-start.3
  246.8 7.3 %copy-start.11 = (s32[4,3]{1,0:T(4,128)S(1)}, s32[4,3]{1,0:T(4,128)}, u32[]{:S(2)}) copy-start(s32[4,3]{1,0:T(4,128)} %param.25) | copy-start | bytes 148
  248.5 16.5 %collective-permute-start.6 = (f32[2,4,128,128]{3,2,1,0:T(8,128)S(1)}, f32[2,4,128,128]{3,2,1,0:T(8,128)S(1)}, u32[]{:S(2)}, u32[]{:S(2)}) collective-permute-start(f32[2,4,128,128]{3,2,1,0:T(8,128)S(1)} %pad_maximum_fusion.3), channel_id=1, source_target_pairs={{0,1},{1,2},{2,3},{3,4},{4,5},{5,6},{6,7},{8,9},{9,10},{10,11},{11... | collective-permute-start | bytes 1572872 | tf_op jit(solution)/shard_map/ppermute | solution.py:38
  252.7 18.3 %collective-permute-start.7 = (f32[2,4,128,128]{3,2,1,0:T(8,128)S(1)}, f32[2,4,128,128]{3,2,1,0:T(8,128)S(1)}, u32[]{:S(2)}, u32[]{:S(2)}) collective-permute-start(f32[2,4,128,128]{3,2,1,0:T(8,128)S(1)} %pad_maximum_fusion.3), channel_id=1, source_target_pairs={{1,0},{2,1},{3,2},{4,3},{5,4},{6,5},{7,6},{9,8},{10,9},{11,10},{12... | collective-permute-start | bytes 1572872 | tf_op jit(solution)/shard_map/ppermute | solution.py:39
Sparse Core Ops, SparseCore 0:
  21.5 33.1 all-gather.2
  189.9 55.5 all-gather.4
